TPU v7x, 32 devices: a whole 2x2x4 slice. The times are simulated.
32 devices in a mesh: dp: 16 (over z, y, x), head: 2 (over core).
Axes of the slice: x: 2, y: 2, z: 4, core: 2. Of those that a mesh axis runs over, the one named last changes fastest.
Arguments:
- hidden: bfloat16 [64, 512, 3584], P(('dp', 'head')), may hold values from -6 to 6
- head_proj: bfloat16 [4, 3584, 128], P('head'), may hold values from -0.09375 to 0.09375
- head_out: bfloat16 [4, 128], P('head'), may hold values from -0.8984375 to 0.8984375
- head_ratio: int32 [4], replicated, may hold values from 2 to 7
- group_of: int32 [64], replicated, may hold values from 0 to 3, as said below
- lengths: int32 [64], P(('dp', 'head')), may hold values from 1 to 512
- token_mask: int32 [64, 512], P(('dp', 'head')), may hold values 0 or 1
Outputs:
- advantages: float32 [64, 512], P(('dp', 'head'))
Inputs may be any that keep to these rules, and one draw needn't show every extreme that they name: `group_of`: every one of the 4 groups holds exactly 16 rollouts.
All inputs are finite; a program needn't handle non-finite values. No bound on the sum of `token_mask` on one device may be relied on, other than what follows from the above.
Results may differ from a plain program's by a relative error of at most 0.0026.
Values may be sent and summed in bfloat16 or wider, within the bound.
No kernel may reach another device: no remote copies, remote signals or barrier semaphores. Data moves between devices by JAX's collectives and lax.ppermute only.
A program may use at most 64 MiB of HBM per device.

v0:
```python
import jax
import jax.numpy as jnp
from jax import lax
from jax.sharding import PartitionSpec as P

GROUP = 16


token_weight = 0.5
gap_weight = 0.5
clip_limit = 2.0
var_offset = 0.04


def head_mixture(head_ratio):
    ratios = head_ratio.astype(jnp.float32)
    return ratios / jnp.sum(ratios)


def mixture_scores(states, projection, readout, mix_weights):
    count_rows, seq_len, model_width = states.shape
    flat_rows = states.reshape(count_rows * seq_len, model_width)
    hidden_pre = jnp.einsum(
        "td,hdr->htr", flat_rows, projection, preferred_element_type=jnp.float32
    )
    active = jnp.tanh(hidden_pre).astype(jnp.bfloat16)
    scores = jnp.einsum("htr,hr->ht", active, readout, preferred_element_type=jnp.float32)
    return jnp.sum(mix_weights[:, None] * scores, axis=0).reshape(count_rows, seq_len)


def on_device(hidden, head_proj, head_out, head_ratio, group_of, lengths, token_mask):
    rollouts, seq_len, model_width = hidden.shape
    mixture = head_mixture(head_ratio)
    combined = mixture_scores(
        hidden,
        lax.all_gather(head_proj, "head", axis=0, tiled=True),
        lax.all_gather(head_out, "head", axis=0, tiled=True),
        mixture,
    )
    positions = jnp.arange(seq_len)
    last_mark = positions[None, :] == (lengths - 1)[:, None]
    reward = jnp.sum(jnp.where(last_mark, combined, 0.0), axis=1)
    group_count = group_of.shape[0] // GROUP
    labels = jnp.arange(group_count)
    start_row = lax.axis_index(("dp", "head")) * rollouts
    my_groups = lax.dynamic_slice_in_dim(group_of, start_row, rollouts)
    member = (my_groups[:, None] == labels[None, :]).astype(jnp.float32)
    everyone = lax.all_gather(reward, ("dp", "head"), axis=0, tiled=True)
    whole_member = (group_of[:, None] == labels[None, :]).astype(jnp.float32)
    group_mean = jnp.sum(whole_member * everyone[:, None], axis=0) / GROUP
    whole_dev = everyone - jnp.sum(whole_member * group_mean[None, :], axis=1)
    group_var = jnp.sum(whole_member * (whole_dev * whole_dev)[:, None], axis=0) / GROUP
    group_best = jnp.max(jnp.where(whole_member > 0, everyone[:, None], -jnp.inf), axis=0)
    mean_rows = jnp.sum(member * group_mean[None, :], axis=1)
    deviation = reward - mean_rows
    var_rows = jnp.sum(member * group_var[None, :], axis=1)
    best_rows = jnp.sum(member * group_best[None, :], axis=1)
    shaped = (
        (deviation / jnp.sqrt(var_rows + var_offset))[:, None]
        + token_weight * combined
        - gap_weight * (best_rows - reward)[:, None]
    )
    valid_mask = (positions[None, :] < lengths[:, None]) & (token_mask == 1)
    return jnp.where(valid_mask, jnp.clip(shaped, -clip_limit, clip_limit), 0.0)


def solution(mesh):
    return jax.shard_map(
        on_device,
        mesh=mesh,
        in_specs=(
            P(("dp", "head"), None, None),
            P("head", None, None),
            P("head", None),
            P(),
            P(),
            P(("dp", "head")),
            P(("dp", "head"), None),
        ),
        out_specs=P(("dp", "head"), None),
        check_vma=False,
    )
```

profile of v0, /device:TPU:0, one launch (start us, length us, event | category | flops | bytes accessed | tf_op | source)
XLA Modules:
  0.0 82.1 jit_solution(8619927760031545544)
XLA Ops:
  6.5 0.0 all-gather.3.cloned.1.call-start
  6.5 0.7 all-gather.3.cloned.1.call-update
  7.3 0.7 dynamic_slice.3
  8.0 2.1 %all-gather = bf16[2,2,128]{2,1,0:T(2,128)(2,1)S(1)} all-gather(bf16[1,2,128]{2,1,0:T(2,128)(2,1)} %bitcast.14), channel_id=1, replica_groups=mesh['dp'=16,'head'=2] {'head'}, dimensions={0}, use_global_device_ids=true | all-gather | bytes 1536 | tf_op jit(solution)/shard_map/all_gather | solution.py:37
  10.1 1.3 %convert_reduce_fusion = f32[]{:T(128)} fusion(s32[4]{0:T(128)} %param.10), kind=kLoop, calls=%fused_computation.22 | loop fusion | flops 7 | bytes 20 | tf_op jit(solution)/shard_map/reduce_sum | solution.py:17
  11.3 1.3 %convert_divide_fusion = f32[4]{0:T(128)S(1)} fusion(s32[4]{0:T(128)} %param.10, f32[]{:T(128)} %convert_reduce_fusion), kind=kLoop, calls=%fused_computation.21 | loop fusion | flops 8 | bytes 36 | tf_op jit(solution)/shard_map/div | solution.py:17
  12.6 0.7 broadcast_add_fusion
  13.3 11.2 %all-gather.3.cloned.1.call-done = bf16[4,3584,128]{2,1,0:T(8,128)(2,1)} async-done(((bf16[2,3584,128]{2,1,0:T(8,128)(2,1)}), bf16[4,3584,128]{2,1,0:T(8,128)(2,1)}) %all-gather.3.cloned.1.call-update) | async-done | bytes 3670032 | tf_op jit(solution)/shard_map/all_gather | solution.py:36
  24.5 0.0 copy-start.2
  24.5 0.0 copy-start
  24.5 0.0 copy-start.1
  24.5 8.4 %fusion = f32[4,1,1024]{2,1,0:T(1,128)S(1)} fusion(bf16[4,3584,128]{2,1,0:T(8,128)(2,1)} %all-gather.3.cloned.1.call-done, bf16[1024,3584,1]{1,0,2:T(8,128)(2,1)} %bitcast.13, bf16[4,128,1]{1,0,2:T(4,128)(2,1)S(1)} %bitcast.15), kind=kOutput, calls=%fused_computation.1 | convolution fusion | flops 3759669248 | bytes 11027456 | tf_op jit(solution)/shard_map/htr,hr->ht/dot_general | solution.py:27
  32.9 0.1 fusion.1
  33.0 0.2 fusion.2
  33.2 0.2 dynamic-update-slice
  33.5 40.5 %all-reduce = f32[64]{0:T(128)S(1)} all-reduce(f32[64]{0:T(128)S(1)} %dynamic-update-slice), channel_id=1, replica_groups=mesh['dp'=16,'head'=2] {'dp','head'}, use_global_device_ids=true, to_apply=%add | all-reduce | flops 64 | bytes 512
  74.0 0.0 copy-done.2
  74.0 0.1 select_reduce_fusion.3
  74.1 0.1 select_reduce_fusion.2
  74.2 0.1 select_reduce_fusion.1
  74.3 0.2 select_reduce_fusion.6
  74.6 0.0 copy-done
  74.6 0.0 copy-done.1
  74.6 0.7 and_select_fusion
  (6 shorter events, 0.0 us)
Async XLA Ops:
  6.5 18.0 %all-gather.3.cloned.1.call-start = ((), (), s32[]{:S(2)}) async-start(), calls=%async_computation | async-start | bytes 5505024 | tf_op jit(solution)/shard_map/all_gather | solution.py:36
  24.5 49.4 %copy-start.2 = (s32[64]{0:T(128)S(1)}, s32[64]{0:T(128)}, u32[]{:S(2)}) copy-start(s32[64]{0:T(128)} %param.11) | copy-start | bytes 772
  24.5 50.0 %copy-start = (s32[2,512]{1,0:T(2,128)S(1)}, s32[2,512]{1,0:T(2,128)}, u32[]{:S(2)}) copy-start(s32[2,512]{1,0:T(2,128)} %param.13) | copy-start | bytes 12292
  24.5 50.0 %copy-start.1 = (s32[2]{0:T(128)S(1)}, s32[2]{0:T(128)}, u32[]{:S(2)}) copy-start(s32[2]{0:T(128)} %param.12) | copy-start | bytes 28
Sparse Core Ops, SparseCore 0:
  8.9 15.6 all-gather.2
where the time goes:
time: 82.4 us; the launch traced here: 82.1 us
  blocking collectives  42.5 us (52%)
  between operations  13.4 us (16%)
  waiting for transfers between devices  11.9 us (14%)
  matrix products  8.41 us (10%)
  other arithmetic  4.75 us (6%)
  local copies, waits for them, and re-layouts  0.99 us (1%)
    unnamed x1, blocking collectives  40.5 us
    all_gather x1, waiting for transfers between devices, on_device(): lax.all_gather(head_proj, 'head', axis=0, tiled=True)  11.2 us
    dot_general x1, matrix products, mixture_scores(): jnp.einsum('htr,hr->ht', active, readout, preferred_element_type=jnp.floa...  8.41 us
    all_gather x1, blocking collectives, on_device(): lax.all_gather(head_out, 'head', axis=0, tiled=True)  2.08 us
  transfers between devices with their start and end apart: 1, of which 1 were waited for; matrix products, arithmetic and copies ran while one was open for 5% of the time, Pallas kernels for 0%

commit v1 on v0

v1 whole, which is shorter than its diff:
```python
import functools

import jax
import jax.numpy as jnp
from jax import lax
from jax.experimental import pallas as pl
from jax.experimental.pallas import tpu as pltpu
from jax.sharding import PartitionSpec as P

GROUP = 16
LANES = 128
ROWS = 16
VMEM_BYTES = 24 << 20

token_weight = 0.5
gap_weight = 0.5
clip_limit = 2.0
var_offset = 0.04

AXES = ("dp", "head")


def tile_rows(seq_len):
    for rows in (256, 128):
        if seq_len % rows == 0:
            return rows
    return seq_len


def tile_scores(states, proj_ref, out_ref, ratio_ref, owner):
    heads = proj_ref.shape[0]
    weights = jnp.concatenate([proj_ref[k] for k in range(heads)], axis=1)
    inner = jnp.dot(states, weights, preferred_element_type=jnp.float32)
    active = jnp.tanh(inner).astype(jnp.bfloat16)
    rank = out_ref.shape[1]
    row = lax.broadcasted_iota(jnp.int32, (ROWS, rank), 0)
    readout = jnp.concatenate(
        [
            jnp.where(row == k, out_ref[k : k + 1, :].astype(jnp.float32), 0.0)
            for k in range(heads)
        ],
        axis=1,
    ).astype(jnp.bfloat16)
    scores = lax.dot_general(
        readout, active, (((1,), (1,)), ((), ())), preferred_element_type=jnp.float32
    )
    total = ratio_ref[0]
    for k in range(1, ratio_ref.shape[0]):
        total = total + ratio_ref[k]
    shape = (1, states.shape[0])
    whole = jnp.full(shape, total, jnp.int32).astype(jnp.float32)
    combined = None
    for k in range(heads):
        share = jnp.full(shape, ratio_ref[owner * heads + k], jnp.int32).astype(jnp.float32)
        term = (share / whole) * scores[k : k + 1, :]
        combined = term if combined is None else combined + term
    return combined


def first_kernel(ratio_ref, hidden_ref, proj_ref, out_ref, part_ref):
    owner = lax.axis_index("head")
    part_ref[...] = tile_scores(hidden_ref[...], proj_ref, out_ref, ratio_ref, owner)


def last_kernel(
    head_size, ratio_ref, group_ref, length_ref, hidden_ref, proj_ref, out_ref, part_ref,
    comb_ref, send_ref,
):
    roll, tile = pl.program_id(0), pl.program_id(1)
    rollouts = pl.num_programs(0)
    head = lax.axis_index("head")
    owner = lax.rem(head + head_size - 1, head_size)
    combined = part_ref[...] + tile_scores(
        hidden_ref[...], proj_ref, out_ref, ratio_ref, owner
    )
    comb_ref[...] = combined
    half = (send_ref.shape[0], 1, LANES)
    lane = lax.broadcasted_iota(jnp.int32, half, 2)

    @pl.when(tile == 0)
    def _():
        me = lax.axis_index("dp") * head_size + head
        mine = jnp.full(half, group_ref[me * rollouts + roll], jnp.int32).astype(jnp.float32)

        @pl.when(roll == 0)
        def _():
            send_ref[:, :, :LANES] = jnp.zeros(half, jnp.float32)
            send_ref[:, :, LANES:] = jnp.full(half, -1.0, jnp.float32)

        send_ref[:, :, LANES:] = jnp.where(lane == roll, mine, send_ref[:, :, LANES:])

    rows = combined.shape[1]
    position = lax.broadcasted_iota(jnp.int32, combined.shape, 1) + tile * rows
    picked = jnp.sum(
        jnp.where(position == length_ref[roll] - 1, combined, 0.0), axis=1, keepdims=True
    )
    send_ref[:, :, :LANES] += jnp.where(lane == roll, picked[None], 0.0)


def finish_kernel(
    head_size, group_ref, length_ref, every_ref, comb_ref, mask_ref, adv_ref
):
    rollouts, _, seq_len = comb_ref.shape
    me = lax.axis_index("dp") * head_size + lax.axis_index("head")
    everyone = every_ref[:, :, :LANES]
    labels = every_ref[:, :, LANES:]

    def over_all(values, op):
        return op(op(values, axis=0), axis=1, keepdims=True)

    position = lax.broadcasted_iota(jnp.int32, (1, seq_len), 1)
    for j in range(rollouts):
        combined = comb_ref[j]
        length = length_ref[j]
        reward = jnp.sum(
            jnp.where(position == length - 1, combined, 0.0), axis=1, keepdims=True
        )
        group = jnp.full(labels.shape, group_ref[me * rollouts + j], jnp.int32)
        member = labels == group.astype(jnp.float32)
        mean = over_all(jnp.where(member, everyone, 0.0), jnp.sum) / GROUP
        gap = everyone - mean[None]
        var = over_all(jnp.where(member, gap * gap, 0.0), jnp.sum) / GROUP
        best = over_all(jnp.where(member, everyone, -jnp.inf), jnp.max)
        base = (reward - mean) / jnp.sqrt(var + var_offset) - gap_weight * (best - reward)
        shaped = jnp.clip(token_weight * combined + base, -clip_limit, clip_limit)
        valid = (position < length) & (mask_ref[j : j + 1, :] == 1)
        adv_ref[j : j + 1, :] = jnp.where(valid, shaped, 0.0)


def smem():
    return pl.BlockSpec(memory_space=pltpu.SMEM)


def vmem():
    return pl.BlockSpec(memory_space=pltpu.VMEM)


def body(dp_size, head_size, hidden, head_proj, head_out, head_ratio, group_of, lengths, token_mask):
    rollouts, seq_len, width = hidden.shape
    heads, _, rank = head_proj.shape
    devices = dp_size * head_size
    rows = tile_rows(seq_len)
    grid = (rollouts, seq_len // rows)

    turn = [
        (d * head_size + h, d * head_size + (h + 1) % head_size)
        for d in range(dp_size)
        for h in range(head_size)
    ]
    other_proj = lax.ppermute(head_proj, AXES, turn)
    other_out = lax.ppermute(head_out, AXES, turn)

    states = pl.BlockSpec((None, rows, width), lambda r, t: (r, t, 0))
    projection = pl.BlockSpec((heads, width, rank), lambda r, t: (0, 0, 0))
    readout = pl.BlockSpec((heads, rank), lambda r, t: (0, 0))
    line = pl.BlockSpec((None, 1, rows), lambda r, t: (r, 0, t))
    line_shape = jax.ShapeDtypeStruct((rollouts, 1, seq_len), jnp.float32)
    tokens = rollouts * seq_len
    cost = pl.CostEstimate(
        flops=2 * tokens * width * heads * rank,
        bytes_accessed=2 * (tokens * width + heads * width * rank),
        transcendentals=tokens * heads * rank,
    )
    params = pltpu.CompilerParams(dimension_semantics=("arbitrary", "arbitrary"), vmem_limit_bytes=VMEM_BYTES
    )
    part = pl.pallas_call(
        first_kernel,
        grid=grid,
        in_specs=[smem(), states, projection, readout],
        out_specs=line,
        out_shape=line_shape,
        cost_estimate=cost,
        compiler_params=params,
        name="own_heads",
    )(head_ratio, hidden, head_proj, head_out)
    combined, send = pl.pallas_call(
        functools.partial(last_kernel, head_size),
        grid=grid,
        in_specs=[smem(), smem(), smem(), states, projection, readout, line],
        out_specs=[line, pl.BlockSpec((devices, 1, 2 * LANES), lambda r, t: (0, 0, 0))],
        out_shape=[line_shape, jax.ShapeDtypeStruct((devices, 1, 2 * LANES), jnp.float32)],
        cost_estimate=cost,
        compiler_params=params,
        name="other_heads",
    )(head_ratio, group_of, lengths, hidden, other_proj, other_out, part)
    everyone = lax.all_to_all(send, AXES, split_axis=0, concat_axis=0, tiled=True)
    return pl.pallas_call(
        functools.partial(finish_kernel, head_size),
        in_specs=[smem(), smem(), vmem(), vmem(), vmem()],
        out_specs=vmem(),
        out_shape=jax.ShapeDtypeStruct((rollouts, seq_len), jnp.float32),
        compiler_params=pltpu.CompilerParams(vmem_limit_bytes=VMEM_BYTES),
        name="advantages",
    )(group_of, lengths, everyone, combined, token_mask)


def solution(mesh):
    dp_size, head_size = mesh.shape["dp"], mesh.shape["head"]
    assert head_size == 2
    return jax.shard_map(
        functools.partial(body, dp_size, head_size),
        mesh=mesh,
        in_specs=(
            P(AXES, None, None),
            P("head", None, None),
            P("head", None),
            P(),
            P(),
            P(AXES),
            P(AXES, None),
        ),
        out_specs=P(AXES, None),
        check_vma=False,
    )
```

time: 82.4 us -> 30.5 us (0.37)
  blocking collectives: 42.5 us -> 14.4 us
  between operations: 13.4 us -> 0.05 us
  waiting for transfers between devices: 11.9 us -> 0.01 us
  Pallas kernels: 0 us -> 9.39 us
  matrix products: 8.41 us -> 0 us
  local copies, waits for them, and re-layouts: 0.99 us -> 5.9 us
  other arithmetic: 4.75 us -> 0 us
    unnamed x1 -> x0, blocking collectives: 40.5 us -> none
    all_to_all x0 -> x1, blocking collectives: none -> 14.4 us  [body(): lax.all_to_all(send, AXES, split_axis=0, concat_axis=0, tiled=True)]
    all_gather x1 -> x0, waiting for transfers between devices: 11.2 us -> none  [on_device(): lax.all_gather(head_proj, 'head', axis=0, tiled=True)]
    pallas_call x0 -> x3, Pallas kernels: none -> 9.39 us  [the longest x1 4.3 us: body(): pl.pallas_call(functools.partial(last_kernel, head_size), grid=grid, in_s...]
    dot_general x1 -> x0, matrix products: 8.41 us -> none  [mixture_scores(): jnp.einsum('htr,hr->ht', active, readout, preferred_element_type=jnp.floa...]
    unnamed x8 -> x14, local copies, waits for them, and re-layouts: 0.25 us -> 5.9 us
    reduce_sum x7 -> x0, other arithmetic: 2.09 us -> none  [the longest x1 1.26 us: head_mixture(): return ratios / jnp.sum(ratios)]
    all_gather x1 -> x0, blocking collectives: 2.08 us -> none  [on_device(): lax.all_gather(head_out, 'head', axis=0, tiled=True)]
  transfers between devices with their start and end apart: 1 -> 2, of which waited for: 1 -> 0; matrix products, arithmetic and copies ran while one was open for 5% -> 0% of each run, Pallas kernels for 0% -> 12%
where the time goes in v1:
time: 30.5 us; the launch traced here: 30.3 us
  blocking collectives  14.4 us (47%)
  Pallas kernels  9.39 us (31%)
  local copies, waits for them, and re-layouts  5.9 us (19%)
  starting transfers between devices  0.51 us (2%)
    all_to_all x1, blocking collectives, body(): lax.all_to_all(send, AXES, split_axis=0, concat_axis=0, tiled=True)  14.4 us
    unnamed x14, local copies, waits for them, and re-layouts  5.9 us
    pallas_call x1, Pallas kernels, body(): pl.pallas_call(functools.partial(last_kernel, head_size), grid=grid, in_s...  4.3 us
    pallas_call x1, Pallas kernels, body(): pl.pallas_call(first_kernel, grid=grid, in_specs=[smem(), states, project...  3.64 us
    pallas_call x1, Pallas kernels, body(): pl.pallas_call(functools.partial(finish_kernel, head_size), in_specs=[sme...  1.45 us
  transfers between devices with their start and end apart: 2, of which 0 were waited for; matrix products, arithmetic and copies ran while one was open for 0% of the time, Pallas kernels for 12%

profile of v1, /device:TPU:0, one launch (start us, length us, event | category | flops | bytes accessed | tf_op | source)
XLA Modules:
  0.0 30.3 jit_solution(7834118855524585643)
XLA Ops:
  0.0 0.5 %collective-permute-start = (bf16[2,3584,128]{2,1,0:T(8,128)(2,1)}, bf16[2,3584,128]{2,1,0:T(8,128)(2,1)S(1)}, u32[]{:S(2)}, u32[]{:S(2)}) collective-permute-start(bf16[2,3584,128]{2,1,0:T(8,128)(2,1)} %proj_ref.1), channel_id=1, source_target_pairs={{0,1},{1,0},{2,3},{3,2},{4,5},{5,4},{6,7},{7,6},{8,9},{9,8},{10,11... | collective-permute-start | bytes 5505032 | tf_op jit(solution)/shard_map/ppermute | solution.py:150
  0.5 0.0 collective-permute-start.1
  0.5 0.0 copy-start
  0.5 3.1 %copy-done = bf16[2,512,3584]{2,1,0:T(8,128)(2,1)S(1)} copy-done((bf16[2,512,3584]{2,1,0:T(8,128)(2,1)S(1)}, bf16[2,512,3584]{2,1,0:T(8,128)(2,1)}, u32[]{:S(2)}) %copy-start) | copy-done | bytes 7340056
  3.6 0.0 copy-start.1
  3.6 1.5 %copy-done.1 = bf16[2,3584,128]{2,1,0:T(8,128)(2,1)S(1)} copy-done((bf16[2,3584,128]{2,1,0:T(8,128)(2,1)S(1)}, bf16[2,3584,128]{2,1,0:T(8,128)(2,1)}, u32[]{:S(2)}) %copy-start.1) | copy-done | bytes 1835032
  5.1 0.0 copy-start.3
  5.1 0.7 %copy-done.3 = s32[4]{0:T(128)S(1)} copy-done((s32[4]{0:T(128)S(1)}, s32[4]{0:T(128)}, u32[]{:S(2)}) %copy-start.3) | copy-done | bytes 40
  5.8 0.0 copy-start.6
  5.8 0.7 %copy-done.6 = bf16[2,128]{1,0:T(2,128)(2,1)S(1)} copy-done((bf16[2,128]{1,0:T(2,128)(2,1)S(1)}, bf16[2,128]{1,0:T(2,128)(2,1)}, u32[]{:S(2)}) %copy-start.6) | copy-done | bytes 536
  6.4 0.0 copy-start.4
  6.4 0.0 copy-start.5
  6.4 3.6 %own_heads.1.part_ref = f32[2,1,512]{2,1,0:T(1,128)S(1)} custom-call(s32[4]{0:T(128)S(1)} %copy-done.3, bf16[2,512,3584]{2,1,0:T(8,128)(2,1)S(1)} %copy-done, bf16[2,3584,128]{2,1,0:T(8,128)(2,1)S(1)} %copy-done.1, bf16[2,128]{1,0:T(2,128)(2,1)S(1)} %copy-done.6), custom_call_target="tpu_custom_call" | custom-call | flops 1879048192 | bytes 9175040 | tf_op jit(solution)/shard_map/own_heads/pallas_call | solution.py:166
  10.1 0.0 copy-start.2
  10.1 0.0 collective-permute-done.1.out_ref
  10.1 0.0 collective-permute-done.proj_ref
  10.1 0.0 copy-done.4
  10.1 0.0 copy-done.5
  10.1 4.3 %other_heads.1 = (f32[2,1,512]{2,1,0:T(1,128)S(1)}, f32[32,1,256]{2,1,0:T(1,128)S(1)}) custom-call(s32[4]{0:T(128)S(1)} %copy-done.3, s32[64]{0:T(128)S(1)} %copy-done.4, s32[2]{0:T(128)S(1)} %copy-done.5, bf16[2,512,3584]{2,1,0:T(8,128)(2,1)S(1)} %copy-done, bf16[2,3584,128]{2,1,0:T(8,128)(2,1)S(1)} %collective-permute-done.proj_ref, ...), custom_call_target="tpu_custom_call" | custom-call | flops 1879048192 | bytes 9175040 | tf_op jit(solution)/shard_map/other_heads/pallas_call | solution.py:176
  14.4 14.4 %all_to_all.5.every_ref = f32[32,1,256]{2,1,0:T(1,128)S(1)} all-to-all(f32[32,1,256]{2,1,0:T(1,128)S(1)} %get-tuple-element.7), channel_id=1, replica_groups=mesh['dp'=16,'head'=2] {'dp','head'}, dimensions={0} | all-to-all | bytes 65536 | tf_op jit(solution)/shard_map/all_to_all | solution.py:186
  28.8 0.0 copy-done.2
  28.8 1.4 %advantages.1 = f32[2,512]{1,0:T(2,128)} custom-call(s32[64]{0:T(128)S(1)} %copy-done.4, s32[2]{0:T(128)S(1)} %copy-done.5, f32[32,1,256]{2,1,0:T(1,128)S(1)} %all_to_all.5.every_ref, f32[2,1,512]{2,1,0:T(1,128)S(1)} %get-tuple-element.8.comb_ref, s32[2,512]{1,0:T(2,128)S(1)} %copy-done.2), custom_call_target="tpu_custom_call" | custom-call | tf_op jit(solution)/shard_map/advantages/pallas_call | solution.py:187
Async XLA Ops:
  0.0 10.1 %collective-permute-start = (bf16[2,3584,128]{2,1,0:T(8,128)(2,1)}, bf16[2,3584,128]{2,1,0:T(8,128)(2,1)S(1)}, u32[]{:S(2)}, u32[]{:S(2)}) collective-permute-start(bf16[2,3584,128]{2,1,0:T(8,128)(2,1)} %proj_ref.1), channel_id=1, source_target_pairs={{0,1},{1,0},{2,3},{3,2},{4,5},{5,4},{6,7},{7,6},{8,9},{9,8},{10,11... | collective-permute-start | bytes 5505032 | tf_op jit(solution)/shard_map/ppermute | solution.py:150
  0.5 9.6 %collective-permute-start.1 = (bf16[2,128]{1,0:T(2,128)(2,1)}, bf16[2,128]{1,0:T(2,128)(2,1)S(1)}, u32[]{:S(2)}, u32[]{:S(2)}) collective-permute-start(bf16[2,128]{1,0:T(2,128)(2,1)} %out_ref.1), channel_id=1, source_target_pairs={{0,1},{1,0},{2,3},{3,2},{4,5},{5,4},{6,7},{7,6},{8,9},{9,8},{10,11... | collective-permute-start | bytes 1544 | tf_op jit(solution)/shard_map/ppermute | solution.py:151
  0.5 3.1 %copy-start = (bf16[2,512,3584]{2,1,0:T(8,128)(2,1)S(1)}, bf16[2,512,3584]{2,1,0:T(8,128)(2,1)}, u32[]{:S(2)}) copy-start(bf16[2,512,3584]{2,1,0:T(8,128)(2,1)} %hidden_ref.3) | copy-start | bytes 22020100
  3.6 1.5 %copy-start.1 = (bf16[2,3584,128]{2,1,0:T(8,128)(2,1)S(1)}, bf16[2,3584,128]{2,1,0:T(8,128)(2,1)}, u32[]{:S(2)}) copy-start(bf16[2,3584,128]{2,1,0:T(8,128)(2,1)} %proj_ref.1) | copy-start | bytes 5505028
  5.1 0.7 %copy-start.3 = (s32[4]{0:T(128)S(1)}, s32[4]{0:T(128)}, u32[]{:S(2)}) copy-start(s32[4]{0:T(128)} %ratio_ref.3) | copy-start | bytes 52
  5.8 0.7 %copy-start.6 = (bf16[2,128]{1,0:T(2,128)(2,1)S(1)}, bf16[2,128]{1,0:T(2,128)(2,1)}, u32[]{:S(2)}) copy-start(bf16[2,128]{1,0:T(2,128)(2,1)} %out_ref.1) | copy-start | bytes 1540
  6.4 3.7 %copy-start.4 = (s32[64]{0:T(128)S(1)}, s32[64]{0:T(128)}, u32[]{:S(2)}) copy-start(s32[64]{0:T(128)} %group_ref.3) | copy-start | bytes 772
  6.4 3.7 %copy-start.5 = (s32[2]{0:T(128)S(1)}, s32[2]{0:T(128)}, u32[]{:S(2)}) copy-start(s32[2]{0:T(128)} %length_ref.3) | copy-start | bytes 28
  10.1 18.8 %copy-start.2 = (s32[2,512]{1,0:T(2,128)S(1)}, s32[2,512]{1,0:T(2,128)}, u32[]{:S(2)}) copy-start(s32[2,512]{1,0:T(2,128)} %mask_ref.1) | copy-start | bytes 12292

commit v2 on v1

--- a/solution.py
+++ b/solution.py
@@ -10,7 +10,7 @@
 GROUP = 16
 LANES = 128
 ROWS = 16
-VMEM_BYTES = 24 << 20
+VMEM_BYTES = 28 << 20
 
 token_weight = 0.5
 gap_weight = 0.5
@@ -21,13 +21,13 @@
 
 
 def tile_rows(seq_len):
-    for rows in (256, 128):
+    for rows in (512, 256, 128):
         if seq_len % rows == 0:
             return rows
     return seq_len
 
 
-def tile_scores(states, proj_ref, out_ref, ratio_ref, owner):
+def tile_scores(states, proj_ref, out_ref):
     heads = proj_ref.shape[0]
     weights = jnp.concatenate([proj_ref[k] for k in range(heads)], axis=1)
     inner = jnp.dot(states, weights, preferred_element_type=jnp.float32)
@@ -41,13 +41,16 @@
         ],
         axis=1,
     ).astype(jnp.bfloat16)
-    scores = lax.dot_general(
+    return lax.dot_general(
         readout, active, (((1,), (1,)), ((), ())), preferred_element_type=jnp.float32
     )
+
+
+def mixed(scores, ratio_ref, owner, heads):
     total = ratio_ref[0]
     for k in range(1, ratio_ref.shape[0]):
         total = total + ratio_ref[k]
-    shape = (1, states.shape[0])
+    shape = (1, scores.shape[1])
     whole = jnp.full(shape, total, jnp.int32).astype(jnp.float32)
     combined = None
     for k in range(heads):
@@ -57,9 +60,9 @@
     return combined
 
 
-def first_kernel(ratio_ref, hidden_ref, proj_ref, out_ref, part_ref):
-    owner = lax.axis_index("head")
-    part_ref[...] = tile_scores(hidden_ref[...], proj_ref, out_ref, ratio_ref, owner)
+def first_kernel(hidden_ref, proj_ref, out_ref, part_ref):
+    scores = tile_scores(hidden_ref[...], proj_ref, out_ref)
+    part_ref[...] = scores[: part_ref.shape[0], :]
 
 
 def last_kernel(
@@ -70,9 +73,10 @@
     rollouts = pl.num_programs(0)
     head = lax.axis_index("head")
     owner = lax.rem(head + head_size - 1, head_size)
-    combined = part_ref[...] + tile_scores(
-        hidden_ref[...], proj_ref, out_ref, ratio_ref, owner
-    )
+    heads = proj_ref.shape[0]
+    scores = tile_scores(hidden_ref[...], proj_ref, out_ref)
+    combined = mixed(part_ref[...], ratio_ref, head, heads)
+    combined = combined + mixed(scores, ratio_ref, owner, heads)
     comb_ref[...] = combined
     half = (send_ref.shape[0], 1, LANES)
     lane = lax.broadcasted_iota(jnp.int32, half, 2)
@@ -154,6 +158,7 @@
     projection = pl.BlockSpec((heads, width, rank), lambda r, t: (0, 0, 0))
     readout = pl.BlockSpec((heads, rank), lambda r, t: (0, 0))
     line = pl.BlockSpec((None, 1, rows), lambda r, t: (r, 0, t))
+    part_line = pl.BlockSpec((None, heads, rows), lambda r, t: (r, 0, t))
     line_shape = jax.ShapeDtypeStruct((rollouts, 1, seq_len), jnp.float32)
     tokens = rollouts * seq_len
     cost = pl.CostEstimate(
@@ -166,17 +171,17 @@
     part = pl.pallas_call(
         first_kernel,
         grid=grid,
-        in_specs=[smem(), states, projection, readout],
-        out_specs=line,
-        out_shape=line_shape,
+        in_specs=[states, projection, readout],
+        out_specs=part_line,
+        out_shape=jax.ShapeDtypeStruct((rollouts, heads, seq_len), jnp.float32),
         cost_estimate=cost,
         compiler_params=params,
         name="own_heads",
-    )(head_ratio, hidden, head_proj, head_out)
+    )(hidden, head_proj, head_out)
     combined, send = pl.pallas_call(
         functools.partial(last_kernel, head_size),
         grid=grid,
-        in_specs=[smem(), smem(), smem(), states, projection, readout, line],
+        in_specs=[smem(), smem(), smem(), states, projection, readout, part_line],
         out_specs=[line, pl.BlockSpec((devices, 1, 2 * LANES), lambda r, t: (0, 0, 0))],
         out_shape=[line_shape, jax.ShapeDtypeStruct((devices, 1, 2 * LANES), jnp.float32)],
         cost_estimate=cost,

time: 30.5 us -> 27.8 us (0.911)
  Pallas kernels: 9.39 us -> 7.41 us
  local copies, waits for them, and re-layouts: 5.9 us -> 5.25 us
    pallas_call x1, Pallas kernels: 3.64 us -> 2.55 us  [body(): pl.pallas_call(first_kernel, grid=grid, in_specs=[states, projection, rea...]
    pallas_call x1, Pallas kernels: 4.3 us -> 3.41 us  [body(): pl.pallas_call(functools.partial(last_kernel, head_size), grid=grid, in_s...]
    unnamed x14, local copies, waits for them, and re-layouts: 5.9 us -> 5.25 us
  transfers between devices with their start and end apart: 2 -> 2, of which waited for: 0 -> 0; matrix products, arithmetic and copies ran while one was open for 0% -> 0% of each run, Pallas kernels for 12% -> 9%
where the time goes in v2:
time: 27.8 us; the launch traced here: 27.6 us
  blocking collectives  14.4 us (52%)
  Pallas kernels  7.41 us (27%)
  local copies, waits for them, and re-layouts  5.25 us (19%)
  starting transfers between devices  0.51 us (2%)
    all_to_all x1, blocking collectives, body(): lax.all_to_all(send, AXES, split_axis=0, concat_axis=0, tiled=True)  14.4 us
    unnamed x14, local copies, waits for them, and re-layouts  5.25 us
    pallas_call x1, Pallas kernels, body(): pl.pallas_call(functools.partial(last_kernel, head_size), grid=grid, in_s...  3.41 us
    pallas_call x1, Pallas kernels, body(): pl.pallas_call(first_kernel, grid=grid, in_specs=[states, projection, rea...  2.55 us
    pallas_call x1, Pallas kernels, body(): pl.pallas_call(functools.partial(finish_kernel, head_size), in_specs=[sme...  1.45 us
  transfers between devices with their start and end apart: 2, of which 0 were waited for; matrix products, arithmetic and copies ran while one was open for 0% of the time, Pallas kernels for 9%

profile of v2, /device:TPU:0, one launch (start us, length us, event | category | flops | bytes accessed | tf_op | source)
XLA Modules:
  0.0 27.6 jit_solution(4035042402327129825)
XLA Ops:
  0.0 0.5 %collective-permute-start = (bf16[2,3584,128]{2,1,0:T(8,128)(2,1)}, bf16[2,3584,128]{2,1,0:T(8,128)(2,1)S(1)}, u32[]{:S(2)}, u32[]{:S(2)}) collective-permute-start(bf16[2,3584,128]{2,1,0:T(8,128)(2,1)} %proj_ref.1), channel_id=1, source_target_pairs={{0,1},{1,0},{2,3},{3,2},{4,5},{5,4},{6,7},{7,6},{8,9},{9,8},{10,11... | collective-permute-start | bytes 5505032 | tf_op jit(solution)/shard_map/ppermute | solution.py:154
  0.5 0.0 collective-permute-start.1
  0.5 0.0 copy-start
  0.5 3.1 %copy-done = bf16[2,512,3584]{2,1,0:T(8,128)(2,1)S(1)} copy-done((bf16[2,512,3584]{2,1,0:T(8,128)(2,1)S(1)}, bf16[2,512,3584]{2,1,0:T(8,128)(2,1)}, u32[]{:S(2)}) %copy-start) | copy-done | bytes 7340056
  3.6 0.0 copy-start.1
  3.6 1.5 %copy-done.1 = bf16[2,3584,128]{2,1,0:T(8,128)(2,1)S(1)} copy-done((bf16[2,3584,128]{2,1,0:T(8,128)(2,1)S(1)}, bf16[2,3584,128]{2,1,0:T(8,128)(2,1)}, u32[]{:S(2)}) %copy-start.1) | copy-done | bytes 1835032
  5.1 0.0 copy-start.5
  5.1 0.7 %copy-done.5 = bf16[2,128]{1,0:T(2,128)(2,1)S(1)} copy-done((bf16[2,128]{1,0:T(2,128)(2,1)S(1)}, bf16[2,128]{1,0:T(2,128)(2,1)}, u32[]{:S(2)}) %copy-start.5) | copy-done | bytes 536
  5.8 0.0 copy-start.3
  5.8 0.0 copy-start.4
  5.8 0.0 copy-start.6
  5.8 2.6 %own_heads.1.part_ref = f32[2,2,512]{2,1,0:T(2,128)S(1)} custom-call(bf16[2,512,3584]{2,1,0:T(8,128)(2,1)S(1)} %copy-done, bf16[2,3584,128]{2,1,0:T(8,128)(2,1)S(1)} %copy-done.1, bf16[2,128]{1,0:T(2,128)(2,1)S(1)} %copy-done.5), custom_call_target="tpu_custom_call" | custom-call | flops 1879048192 | bytes 9175040 | tf_op jit(solution)/shard_map/own_heads/pallas_call | solution.py:171
  8.3 0.0 copy-start.2
  8.3 0.0 collective-permute-done.1.out_ref
  8.3 0.0 collective-permute-done.proj_ref
  8.3 0.0 copy-done.3
  8.3 0.0 copy-done.4
  8.4 0.0 copy-done.6
  8.4 3.4 %other_heads.1 = (f32[2,1,512]{2,1,0:T(1,128)S(1)}, f32[32,1,256]{2,1,0:T(1,128)S(1)}) custom-call(s32[4]{0:T(128)S(1)} %copy-done.6, s32[64]{0:T(128)S(1)} %copy-done.3, s32[2]{0:T(128)S(1)} %copy-done.4, bf16[2,512,3584]{2,1,0:T(8,128)(2,1)S(1)} %copy-done, bf16[2,3584,128]{2,1,0:T(8,128)(2,1)S(1)} %collective-permute-done.proj_ref, ...), custom_call_target="tpu_custom_call" | custom-call | flops 1879048192 | bytes 9175040 | tf_op jit(solution)/shard_map/other_heads/pallas_call | solution.py:181
  11.8 14.4 %all_to_all.5.every_ref = f32[32,1,256]{2,1,0:T(1,128)S(1)} all-to-all(f32[32,1,256]{2,1,0:T(1,128)S(1)} %get-tuple-element.7), channel_id=1, replica_groups=mesh['dp'=16,'head'=2] {'dp','head'}, dimensions={0} | all-to-all | bytes 65536 | tf_op jit(solution)/shard_map/all_to_all | solution.py:191
  26.2 0.0 copy-done.2
  26.2 1.4 %advantages.1 = f32[2,512]{1,0:T(2,128)} custom-call(s32[64]{0:T(128)S(1)} %copy-done.3, s32[2]{0:T(128)S(1)} %copy-done.4, f32[32,1,256]{2,1,0:T(1,128)S(1)} %all_to_all.5.every_ref, f32[2,1,512]{2,1,0:T(1,128)S(1)} %get-tuple-element.8.comb_ref, s32[2,512]{1,0:T(2,128)S(1)} %copy-done.2), custom_call_target="tpu_custom_call" | custom-call | tf_op jit(solution)/shard_map/advantages/pallas_call | solution.py:192
Async XLA Ops:
  0.0 8.3 %collective-permute-start = (bf16[2,3584,128]{2,1,0:T(8,128)(2,1)}, bf16[2,3584,128]{2,1,0:T(8,128)(2,1)S(1)}, u32[]{:S(2)}, u32[]{:S(2)}) collective-permute-start(bf16[2,3584,128]{2,1,0:T(8,128)(2,1)} %proj_ref.1), channel_id=1, source_target_pairs={{0,1},{1,0},{2,3},{3,2},{4,5},{5,4},{6,7},{7,6},{8,9},{9,8},{10,11... | collective-permute-start | bytes 5505032 | tf_op jit(solution)/shard_map/ppermute | solution.py:154
  0.5 7.8 %collective-permute-start.1 = (bf16[2,128]{1,0:T(2,128)(2,1)}, bf16[2,128]{1,0:T(2,128)(2,1)S(1)}, u32[]{:S(2)}, u32[]{:S(2)}) collective-permute-start(bf16[2,128]{1,0:T(2,128)(2,1)} %out_ref.1), channel_id=1, source_target_pairs={{0,1},{1,0},{2,3},{3,2},{4,5},{5,4},{6,7},{7,6},{8,9},{9,8},{10,11... | collective-permute-start | bytes 1544 | tf_op jit(solution)/shard_map/ppermute | solution.py:155
  0.5 3.1 %copy-start = (bf16[2,512,3584]{2,1,0:T(8,128)(2,1)S(1)}, bf16[2,512,3584]{2,1,0:T(8,128)(2,1)}, u32[]{:S(2)}) copy-start(bf16[2,512,3584]{2,1,0:T(8,128)(2,1)} %hidden_ref.3) | copy-start | bytes 22020100
  3.6 1.5 %copy-start.1 = (bf16[2,3584,128]{2,1,0:T(8,128)(2,1)S(1)}, bf16[2,3584,128]{2,1,0:T(8,128)(2,1)}, u32[]{:S(2)}) copy-start(bf16[2,3584,128]{2,1,0:T(8,128)(2,1)} %proj_ref.1) | copy-start | bytes 5505028
  5.1 0.7 %copy-start.5 = (bf16[2,128]{1,0:T(2,128)(2,1)S(1)}, bf16[2,128]{1,0:T(2,128)(2,1)}, u32[]{:S(2)}) copy-start(bf16[2,128]{1,0:T(2,128)(2,1)} %out_ref.1) | copy-start | bytes 1540
  5.8 2.6 %copy-start.3 = (s32[64]{0:T(128)S(1)}, s32[64]{0:T(128)}, u32[]{:S(2)}) copy-start(s32[64]{0:T(128)} %group_ref.3) | copy-start | bytes 772
  5.8 2.6 %copy-start.4 = (s32[2]{0:T(128)S(1)}, s32[2]{0:T(128)}, u32[]{:S(2)}) copy-start(s32[2]{0:T(128)} %length_ref.3) | copy-start | bytes 28
  5.8 2.6 %copy-start.6 = (s32[4]{0:T(128)S(1)}, s32[4]{0:T(128)}, u32[]{:S(2)}) copy-start(s32[4]{0:T(128)} %ratio_ref.1) | copy-start | bytes 52
  8.3 17.9 %copy-start.2 = (s32[2,512]{1,0:T(2,128)S(1)}, s32[2,512]{1,0:T(2,128)}, u32[]{:S(2)}) copy-start(s32[2,512]{1,0:T(2,128)} %mask_ref.1) | copy-start | bytes 12292

commit v3 on v2

--- a/solution.py
+++ b/solution.py
@@ -11,6 +11,7 @@
 LANES = 128
 ROWS = 16
 VMEM_BYTES = 28 << 20
+OWN_BYTES = 55600 << 10
 
 token_weight = 0.5
 gap_weight = 0.5
@@ -175,7 +176,9 @@
         out_specs=part_line,
         out_shape=jax.ShapeDtypeStruct((rollouts, heads, seq_len), jnp.float32),
         cost_estimate=cost,
-        compiler_params=params,
+        compiler_params=pltpu.CompilerParams(
+            dimension_semantics=("arbitrary", "arbitrary"), vmem_limit_bytes=OWN_BYTES
+        ),
         name="own_heads",
     )(hidden, head_proj, head_out)
     combined, send = pl.pallas_call(

time: 27.8 us -> 26.7 us (0.960)
  local copies, waits for them, and re-layouts: 5.25 us -> 0.71 us
  Pallas kernels: 7.41 us -> 10.7 us
    unnamed x14 -> x12, local copies, waits for them, and re-layouts: 5.25 us -> 0.71 us
    pallas_call x1, Pallas kernels: 2.55 us -> 5.93 us  [body(): pl.pallas_call(first_kernel, grid=grid, in_specs=[states, projection, rea...]
  transfers between devices with their start and end apart: 2 -> 2, of which waited for: 0 -> 0; matrix products, arithmetic and copies ran while one was open for 0% -> 0% of each run, Pallas kernels for 9% -> 22%
where the time goes in v3:
time: 26.7 us; the launch traced here: 26.5 us
  blocking collectives  14.3 us (54%)
  Pallas kernels  10.7 us (40%)
  local copies, waits for them, and re-layouts  0.71 us (3%)
  starting transfers between devices  0.64 us (2%)
    all_to_all x1, blocking collectives, body(): lax.all_to_all(send, AXES, split_axis=0, concat_axis=0, tiled=True)  14.3 us
    pallas_call x1, Pallas kernels, body(): pl.pallas_call(first_kernel, grid=grid, in_specs=[states, projection, rea...  5.93 us
    pallas_call x1, Pallas kernels, body(): pl.pallas_call(functools.partial(last_kernel, head_size), grid=grid, in_s...  3.35 us
    pallas_call x1, Pallas kernels, body(): pl.pallas_call(functools.partial(finish_kernel, head_size), in_specs=[sme...  1.45 us
    unnamed x12, local copies, waits for them, and re-layouts  0.71 us
    ppermute x1, starting transfers between devices, body(): other_proj = lax.ppermute(head_proj, AXES, turn)  0.56 us
  transfers between devices with their start and end apart: 2, of which 0 were waited for; matrix products, arithmetic and copies ran while one was open for 0% of the time, Pallas kernels for 22%

profile of v3, /device:TPU:0, one launch (start us, length us, event | category | flops | bytes accessed | tf_op | source)
XLA Modules:
  0.0 26.5 jit_solution(4918320193466790773)
XLA Ops:
  0.0 0.0 copy-start.4
  0.0 0.0 copy-start.3
  0.0 0.0 copy-start.5
  0.0 0.6 %collective-permute-start = (bf16[2,3584,128]{2,1,0:T(8,128)(2,1)}, bf16[2,3584,128]{2,1,0:T(8,128)(2,1)S(1)}, u32[]{:S(2)}, u32[]{:S(2)}) collective-permute-start(bf16[2,3584,128]{2,1,0:T(8,128)(2,1)} %proj_ref.1), channel_id=1, source_target_pairs={{0,1},{1,0},{2,3},{3,2},{4,5},{5,4},{6,7},{7,6},{8,9},{9,8},{10,11... | collective-permute-start | bytes 5505032 | tf_op jit(solution)/shard_map/ppermute | solution.py:155
  0.6 0.1 collective-permute-start.1
  0.6 0.0 copy-start
  0.6 0.0 copy-start.2
  0.7 5.9 %own_heads.1.part_ref = f32[2,2,512]{2,1,0:T(2,128)} custom-call(bf16[2,512,3584]{2,1,0:T(8,128)(2,1)} %hidden_ref.3, bf16[2,3584,128]{2,1,0:T(8,128)(2,1)} %proj_ref.1, bf16[2,128]{1,0:T(2,128)(2,1)} %out_ref.1), custom_call_target="tpu_custom_call" | custom-call | flops 1879048192 | bytes 9175040 | tf_op jit(solution)/shard_map/own_heads/pallas_call | solution.py:172
  6.6 0.0 collective-permute-done.1.out_ref
  6.6 0.0 collective-permute-done.proj_ref
  6.6 0.0 copy-done.4
  6.6 0.0 copy-done.3
  6.6 0.0 copy-done.5
  6.6 0.0 copy-done
  6.6 0.0 copy-start.1
  6.6 0.7 %copy-done.1 = f32[2,2,512]{2,1,0:T(2,128)S(1)} copy-done((f32[2,2,512]{2,1,0:T(2,128)S(1)}, f32[2,2,512]{2,1,0:T(2,128)}, u32[]{:S(2)}) %copy-start.1) | copy-done | bytes 8216
  7.3 3.3 %other_heads.1 = (f32[2,1,512]{2,1,0:T(1,128)S(1)}, f32[32,1,256]{2,1,0:T(1,128)S(1)}) custom-call(s32[4]{0:T(128)S(1)} %copy-done.5, s32[64]{0:T(128)S(1)} %copy-done.3, s32[2]{0:T(128)S(1)} %copy-done.4, bf16[2,512,3584]{2,1,0:T(8,128)(2,1)S(1)} %copy-done, bf16[2,3584,128]{2,1,0:T(8,128)(2,1)S(1)} %collective-permute-done.proj_ref, ...), custom_call_target="tpu_custom_call" | custom-call | flops 1879048192 | bytes 9175040 | tf_op jit(solution)/shard_map/other_heads/pallas_call | solution.py:184
  10.7 14.3 %all_to_all.5.every_ref = f32[32,1,256]{2,1,0:T(1,128)S(1)} all-to-all(f32[32,1,256]{2,1,0:T(1,128)S(1)} %get-tuple-element.7), channel_id=1, replica_groups=mesh['dp'=16,'head'=2] {'dp','head'}, dimensions={0} | all-to-all | bytes 65536 | tf_op jit(solution)/shard_map/all_to_all | solution.py:194
  25.0 0.0 copy-done.2
  25.0 1.4 %advantages.1 = f32[2,512]{1,0:T(2,128)} custom-call(s32[64]{0:T(128)S(1)} %copy-done.3, s32[2]{0:T(128)S(1)} %copy-done.4, f32[32,1,256]{2,1,0:T(1,128)S(1)} %all_to_all.5.every_ref, f32[2,1,512]{2,1,0:T(1,128)S(1)} %get-tuple-element.8.comb_ref, s32[2,512]{1,0:T(2,128)S(1)} %copy-done.2), custom_call_target="tpu_custom_call" | custom-call | tf_op jit(solution)/shard_map/advantages/pallas_call | solution.py:195
Async XLA Ops:
  0.0 6.6 %copy-start.4 = (s32[2]{0:T(128)S(1)}, s32[2]{0:T(128)}, u32[]{:S(2)}) copy-start(s32[2]{0:T(128)} %length_ref.3) | copy-start | bytes 28
  0.0 6.6 %copy-start.3 = (s32[64]{0:T(128)S(1)}, s32[64]{0:T(128)}, u32[]{:S(2)}) copy-start(s32[64]{0:T(128)} %group_ref.3) | copy-start | bytes 772
  0.0 6.6 %copy-start.5 = (s32[4]{0:T(128)S(1)}, s32[4]{0:T(128)}, u32[]{:S(2)}) copy-start(s32[4]{0:T(128)} %ratio_ref.1) | copy-start | bytes 52
  0.0 6.6 %collective-permute-start = (bf16[2,3584,128]{2,1,0:T(8,128)(2,1)}, bf16[2,3584,128]{2,1,0:T(8,128)(2,1)S(1)}, u32[]{:S(2)}, u32[]{:S(2)}) collective-permute-start(bf16[2,3584,128]{2,1,0:T(8,128)(2,1)} %proj_ref.1), channel_id=1, source_target_pairs={{0,1},{1,0},{2,3},{3,2},{4,5},{5,4},{6,7},{7,6},{8,9},{9,8},{10,11... | collective-permute-start | bytes 5505032 | tf_op jit(solution)/shard_map/ppermute | solution.py:155
  0.6 6.0 %collective-permute-start.1 = (bf16[2,128]{1,0:T(2,128)(2,1)}, bf16[2,128]{1,0:T(2,128)(2,1)S(1)}, u32[]{:S(2)}, u32[]{:S(2)}) collective-permute-start(bf16[2,128]{1,0:T(2,128)(2,1)} %out_ref.1), channel_id=1, source_target_pairs={{0,1},{1,0},{2,3},{3,2},{4,5},{5,4},{6,7},{7,6},{8,9},{9,8},{10,11... | collective-permute-start | bytes 1544 | tf_op jit(solution)/shard_map/ppermute | solution.py:156
  0.6 6.0 %copy-start = (bf16[2,512,3584]{2,1,0:T(8,128)(2,1)S(1)}, bf16[2,512,3584]{2,1,0:T(8,128)(2,1)}, u32[]{:S(2)}) copy-start(bf16[2,512,3584]{2,1,0:T(8,128)(2,1)} %hidden_ref.3) | copy-start | bytes 22020100
  0.6 24.4 %copy-start.2 = (s32[2,512]{1,0:T(2,128)S(1)}, s32[2,512]{1,0:T(2,128)}, u32[]{:S(2)}) copy-start(s32[2,512]{1,0:T(2,128)} %mask_ref.1) | copy-start | bytes 12292
  6.6 0.7 %copy-start.1 = (f32[2,2,512]{2,1,0:T(2,128)S(1)}, f32[2,2,512]{2,1,0:T(2,128)}, u32[]{:S(2)}) copy-start(f32[2,2,512]{2,1,0:T(2,128)} %own_heads.1.part_ref) | copy-start | bytes 24580
